TPU v7x, 128 devices: a whole 4x4x4 slice. The times are simulated.
128 devices in a mesh: rep: 16 (over y_hi, z, core), tp: 8 (over y_lo, x).
Axes of the slice: x: 4, y: 4 (y_hi: 2, y_lo: 2; y = y_hi * 2 + y_lo), z: 4, core: 2. Of those that a mesh axis runs over, the one named last changes fastest.
Arguments:
- delta_query: bfloat16 [16, 2, 2048, 3072], P('rep', None, None, 'tp'), may hold values from -6 to 6
- master_query: float32 [2, 2048, 3072], P(None, 'rep', 'tp'), may hold values from -3 to 3
- moment_query: float32 [2, 2048, 3072], P(None, 'rep', 'tp'), may hold values from -3 to 3
- delta_latent: bfloat16 [16, 2, 512, 4096], P('rep', None, None, 'tp'), may hold values from -6 to 6
- master_latent: float32 [2, 512, 4096], P(None, 'rep', 'tp'), may hold values from -3 to 3
- moment_latent: float32 [2, 512, 4096], P(None, 'rep', 'tp'), may hold values from -3 to 3
- delta_output: bfloat16 [16, 2, 2048, 2048], P('rep', None, 'tp'), may hold values from -6 to 6
- master_output: float32 [2, 2048, 2048], P(None, 'tp', 'rep'), may hold values from -3 to 3
- moment_output: float32 [2, 2048, 2048], P(None, 'tp', 'rep'), may hold values from -3 to 3
Outputs:
- params_query: bfloat16 [2, 2048, 3072], P(None, None, 'tp')
- new_master_query: float32 [2, 2048, 3072], P(None, 'rep', 'tp')
- new_moment_query: float32 [2, 2048, 3072], P(None, 'rep', 'tp')
- params_latent: bfloat16 [2, 512, 4096], P(None, None, 'tp')
- new_master_latent: float32 [2, 512, 4096], P(None, 'rep', 'tp')
- new_moment_latent: float32 [2, 512, 4096], P(None, 'rep', 'tp')
- params_output: bfloat16 [2, 2048, 2048], P(None, 'tp')
- new_master_output: float32 [2, 2048, 2048], P(None, 'tp', 'rep')
- new_moment_output: float32 [2, 2048, 2048], P(None, 'tp', 'rep')
All inputs are finite; a program needn't handle non-finite values.
Results may differ from a plain program's by a relative error of at most 0.012.
Values may be sent and summed in bfloat16 or wider, within the bound.
A program may use at most 64 MiB of HBM per device.

v0:
```python
import jax
import jax.numpy as jnp
from jax import lax
from jax.sharding import Mesh
from jax.sharding import PartitionSpec as P

REP = ("rep_0", "rep_1", "rep_2")
OUTER_RATE = 0.7
OUTER_MOMENTUM = 0.9


def in_blocks(value, dim, length):
    lengths = value.shape
    blocks = value.reshape(*lengths[:dim], length, lengths[dim] // length, *lengths[dim + 1 :])
    return jnp.moveaxis(blocks, dim, 0)


def joined_along(blocks, dim):
    lengths = list(blocks.shape[1:])
    lengths[dim] *= blocks.shape[0]
    return jnp.moveaxis(blocks, 0, dim).reshape(lengths)


def moved_by_axis(blocks, axes, order):
    inside = blocks.shape[1:]
    out = blocks.reshape(*(lax.axis_size(a) for a in axes), *inside)
    for k in order:
        out = lax.all_to_all(out, axes[k], k, k, tiled=True)
    return out.reshape(-1, *inside)


def core_and_chips(value, groups, order, split_dim, concat_dim):
    length = lax.axis_size(groups[0]) * lax.axis_size(groups[1])
    blocks = in_blocks(value, split_dim, length)
    return joined_along(moved_by_axis(blocks, groups, order), concat_dim)


def copy_for_each(value, axis):
    length = lax.axis_size(axis)
    return lax.all_to_all(
        jnp.broadcast_to(value[None], (length, *value.shape)), axis, 0, 0, tiled=True
    )


def gathered_copies(value, axis, dim):
    blocks = copy_for_each(value, axis)
    return joined_along(blocks, dim)


def nesterov(totals, master, moment, replica_count):
    average = totals / replica_count
    momentum = OUTER_MOMENTUM * moment + average
    updated = master - OUTER_RATE * (average + OUTER_MOMENTUM * momentum)
    return (updated, momentum)


def outer_step(
    delta_query,
    master_query,
    moment_query,
    delta_latent,
    master_latent,
    moment_latent,
    delta_output,
    master_output,
    moment_output,
):
    replica_count = lax.axis_size(REP)
    query_terms = core_and_chips(delta_query, (("rep_0", "rep_1"), "rep_2"), (1, 0), 2, 0)
    latent_terms = lax.all_to_all(delta_latent, REP, split_axis=2, concat_axis=0, tiled=True)
    output_terms = lax.all_to_all(delta_output, REP, split_axis=3, concat_axis=0, tiled=True)
    query_totals = jnp.sum(query_terms.astype(jnp.float32), 0)
    latent_totals = jnp.sum(latent_terms.astype(jnp.float32), 0)
    output_totals = jnp.sum(output_terms.astype(jnp.float32), 0)
    query_master, query_moment = nesterov(query_totals, master_query, moment_query, replica_count)
    latent_master, latent_moment = nesterov(
        latent_totals, master_latent, moment_latent, replica_count
    )
    output_master, output_moment = nesterov(
        output_totals, master_output, moment_output, replica_count
    )
    query_params = lax.all_gather(query_master.astype(jnp.bfloat16), REP, axis=1, tiled=True)
    latent_params = gathered_copies(latent_master.astype(jnp.bfloat16), REP, 1)
    output_params = lax.all_gather(output_master.astype(jnp.bfloat16), REP, axis=2, tiled=True)
    return (
        query_params,
        query_master,
        query_moment,
        latent_params,
        latent_master,
        latent_moment,
        output_params,
        output_master,
        output_moment,
    )


def on_device(
    delta_query,
    master_query,
    moment_query,
    delta_latent,
    master_latent,
    moment_latent,
    delta_output,
    master_output,
    moment_output,
):
    return outer_step(
        delta_query,
        master_query,
        moment_query,
        delta_latent,
        master_latent,
        moment_latent,
        delta_output,
        master_output,
        moment_output,
    )


def solution(mesh):
    torus = Mesh(mesh.devices.reshape(2, 4, 2, mesh.shape["tp"]), ("rep_0", "rep_1", "rep_2", "tp"))
    return jax.shard_map(
        on_device,
        mesh=torus,
        in_specs=(
            P(REP, None, None, "tp"),
            P(None, REP, "tp"),
            P(None, REP, "tp"),
            P(REP, None, None, "tp"),
            P(None, REP, "tp"),
            P(None, REP, "tp"),
            P(REP, None, "tp", None),
            P(None, "tp", REP),
            P(None, "tp", REP),
        ),
        out_specs=(
            P(None, None, "tp"),
            P(None, REP, "tp"),
            P(None, REP, "tp"),
            P(None, None, "tp"),
            P(None, REP, "tp"),
            P(None, REP, "tp"),
            P(None, "tp", None),
            P(None, "tp", REP),
            P(None, "tp", REP),
        ),
        check_vma=False,
    )
```

profile of v0, /device:TPU:1, one launch (start us, length us, event | category | flops | bytes accessed | tf_op | source)
XLA Modules:
  0.0 191.4 jit_solution(4195767868516132089)
XLA Ops:
  7.2 0.0 copy-start.3
  7.2 6.2 %copy.70 = bf16[1,2,256,2048]{2,1,0,3:T(2,128)(2,1)} copy(bf16[1,2,256,2048]{3,2,1,0:T(8,128)(2,1)} %param.15) | data formatting | bytes 4194304 | tf_op args[6]
  13.4 0.0 copy-start.4
  13.4 9.6 %all-to-all-start.4 = ((bf16[1,2,256,2048]{2,1,0,3:T(2,128)(2,1)}), bf16[1,2,256,2048]{2,1,0,3:T(2,128)(2,1)S(1)}, u32[]{:S(2)}, u32[]{:S(2)}) async-start(bf16[1,2,256,2048]{2,1,0,3:T(2,128)(2,1)} %copy.70), calls=%async_computation.4 | async-start | bytes 4194304 | tf_op jit(solution)/shard_map/all_to_all | solution.py:71
  23.0 0.0 all-gather.5.cloned.1.call-start
  23.0 0.0 copy-done.3
  23.0 0.1 copy.71
  23.2 0.0 copy-done.4
  23.2 0.1 copy.72
  23.3 28.0 %all-to-all-done.4 = bf16[1,2,256,2048]{2,1,0,3:T(2,128)(2,1)S(1)} async-done(((bf16[1,2,256,2048]{2,1,0,3:T(2,128)(2,1)}), bf16[1,2,256,2048]{2,1,0,3:T(2,128)(2,1)S(1)}, u32[]{:S(2)}, u32[]{:S(2)}) %all-to-all-start.4) | async-done | bytes 2097184 | tf_op jit(solution)/shard_map/all_to_all | solution.py:71
  51.3 1.8 convert_reduce_fusion.1
  53.1 1.1 fusion
  54.2 0.0 all-gather.5.cloned.1.call-update
  54.2 0.0 all-gather.3.cloned.1.call-start
  54.2 2.4 %copy.65 = bf16[8,2,1,2,128,384]{5,4,0,3,2,1:T(8,128)(2,1)S(1)} copy(bf16[8,2,1,2,128,384]{5,4,1,0,3,2:T(8,128)(2,1)} %bitcast.14) | data formatting | bytes 6291456 | tf_op jit(solution)/shard_map/reshape | solution.py:26
  56.6 6.9 %all_to_all.33 = bf16[8,2,1,2,128,384]{5,4,0,3,2,1:T(8,128)(2,1)S(1)} all-to-all(bf16[8,2,1,2,128,384]{5,4,0,3,2,1:T(8,128)(2,1)S(1)} %copy.65), channel_id=1, replica_groups=mesh['rep_0'=2,'rep_1'=4,'rep_2'=2,'tp'=8] {'rep_2'}, dimensions={1} | all-to-all | bytes 6291456 | tf_op jit(solution)/shard_map/all_to_all | solution.py:28
  63.6 0.5 copy.66
  64.1 49.1 %all_to_all.34 = bf16[8,2,1,2,128,384]{5,4,1,3,2,0:T(8,128)(2,1)S(1)} all-to-all(bf16[8,2,1,2,128,384]{5,4,1,3,2,0:T(8,128)(2,1)S(1)} %copy.66), channel_id=1, replica_groups=mesh['rep_0'=2,'rep_1'=4,'rep_2'=2,'tp'=8] {'rep_0','rep_1'}, dimensions={0} | all-to-all | bytes 6291456 | tf_op jit(solution)/shard_map/all_to_all | solution.py:28
  113.2 0.0 copy-start.1
  113.2 0.0 copy-start.2
  113.2 0.0 copy-start
  113.2 0.4 convert_reduce_fusion
  113.7 0.6 copy-done.1
  114.2 0.1 copy-done.2
  114.3 1.0 fusion.2
  115.4 0.0 copy-start.5
  115.4 0.0 copy-start.6
  115.4 0.0 all-gather.3.cloned.1.call-update
  115.4 0.0 copy-done
  115.4 1.1 copy.67
  116.5 23.9 %all_to_all.35 = bf16[1,2,512,512]{3,1,0,2:T(2,128)(2,1)S(1)} all-to-all(bf16[1,2,512,512]{3,1,0,2:T(2,128)(2,1)S(1)} %copy.67), channel_id=1, replica_groups=mesh['rep_0'=2,'rep_1'=4,'rep_2'=2,'tp'=8] {'rep_0','rep_1','rep_2'}, dimensions={2} | all-to-all | bytes 2097152 | tf_op jit(solution)/shard_map/all_to_all | solution.py:70
  140.4 0.9 convert_reduce_fusion.2
  141.3 0.0 copy-done.5
  141.3 0.0 copy-done.6
  141.3 0.8 fusion.1
  142.0 1.1 broadcast_in_dim.2
  143.1 4.7 %all-to-all-start.3 = ((bf16[16,2,32,512]{3,2,1,0:T(8,128)(2,1)}), bf16[16,2,32,512]{3,2,1,0:T(8,128)(2,1)S(1)}, u32[]{:S(2)}, u32[]{:S(2)}) async-start(bf16[16,2,32,512]{3,2,1,0:T(8,128)(2,1)} %broadcast_in_dim.2), calls=%async_computation.3 | async-start | bytes 2097152 | tf_op jit(solution)/shard_map/all_to_all | solution.py:40
  147.8 0.8 copy.74
  148.7 0.8 copy.75
  149.5 23.9 %all-to-all-done.3 = bf16[16,2,32,512]{3,2,1,0:T(8,128)(2,1)S(1)} async-done(((bf16[16,2,32,512]{3,2,1,0:T(8,128)(2,1)}), bf16[16,2,32,512]{3,2,1,0:T(8,128)(2,1)S(1)}, u32[]{:S(2)}, u32[]{:S(2)}) %all-to-all-start.3) | async-done | bytes 1048608 | tf_op jit(solution)/shard_map/all_to_all | solution.py:40
  173.4 1.0 copy.69
  174.5 0.0 all-gather.5.cloned.1.call-done
  174.5 6.2 %copy.73 = bf16[2,256,2048]{2,1,0:T(8,128)(2,1)} copy(bf16[2,256,2048]{1,0,2:T(2,128)(2,1)} %all-gather.5.cloned.1.call-done) | data formatting | bytes 4194304
  180.7 0.0 all-gather.3.cloned.1.call-done
  180.7 3.9 %copy.86 = bf16[2,2048,384]{2,1,0:T(8,128)(2,1)} copy(bf16[2,2048,384]{2,1,0:T(8,128)(2,1)} %all-gather.3.cloned.1.call-done) | data formatting | bytes 6291456
Async XLA Ops:
  7.2 15.8 %copy-start.3 = (f32[2,256,128]{2,1,0:T(8,128)S(1)}, f32[2,256,128]{2,1,0:T(8,128)}, u32[]{:S(2)}) copy-start(f32[2,256,128]{2,1,0:T(8,128)} %param.17) | copy-start | bytes 786436
  13.4 9.8 %copy-start.4 = (f32[2,256,128]{2,1,0:T(8,128)S(1)}, f32[2,256,128]{2,1,0:T(8,128)}, u32[]{:S(2)}) copy-start(f32[2,256,128]{2,1,0:T(8,128)} %param.16) | copy-start | bytes 786436
  13.4 37.9 %all-to-all-start.4 = ((bf16[1,2,256,2048]{2,1,0,3:T(2,128)(2,1)}), bf16[1,2,256,2048]{2,1,0,3:T(2,128)(2,1)S(1)}, u32[]{:S(2)}, u32[]{:S(2)}) async-start(bf16[1,2,256,2048]{2,1,0,3:T(2,128)(2,1)} %copy.70), calls=%async_computation.4 | async-start | bytes 4194304 | tf_op jit(solution)/shard_map/all_to_all | solution.py:71
  23.0 151.5 %all-gather.5.cloned.1.call-start = ((), (), s32[]{:S(2)}) async-start(), calls=%async_computation.6 | async-start | bytes 2228224 | tf_op jit(solution)/shard_map/all_gather | solution.py:84
  54.2 126.5 %all-gather.3.cloned.1.call-start = ((), (), s32[]{:S(2)}) async-start(), calls=%async_computation.5 | async-start | bytes 3342336 | tf_op jit(solution)/shard_map/all_gather | solution.py:82
  113.2 1.0 copy-start.1
  113.2 1.1 copy-start.2
  113.2 2.2 %copy-start = (bf16[1,2,512,512]{3,2,1,0:T(8,128)(2,1)S(1)}, bf16[1,2,512,512]{3,2,1,0:T(8,128)(2,1)}, u32[]{:S(2)}) copy-start(bf16[1,2,512,512]{3,2,1,0:T(8,128)(2,1)} %param.12) | copy-start | bytes 3145732
  115.4 25.9 %copy-start.5 = (f32[2,32,512]{2,1,0:T(8,128)S(1)}, f32[2,32,512]{2,1,0:T(8,128)}, u32[]{:S(2)}) copy-start(f32[2,32,512]{2,1,0:T(8,128)} %param.13) | copy-start | bytes 393220
  115.4 25.9 %copy-start.6 = (f32[2,32,512]{2,1,0:T(8,128)S(1)}, f32[2,32,512]{2,1,0:T(8,128)}, u32[]{:S(2)}) copy-start(f32[2,32,512]{2,1,0:T(8,128)} %param.14) | copy-start | bytes 393220
  143.1 30.3 %all-to-all-start.3 = ((bf16[16,2,32,512]{3,2,1,0:T(8,128)(2,1)}), bf16[16,2,32,512]{3,2,1,0:T(8,128)(2,1)S(1)}, u32[]{:S(2)}, u32[]{:S(2)}) async-start(bf16[16,2,32,512]{3,2,1,0:T(8,128)(2,1)} %broadcast_in_dim.2), calls=%async_computation.3 | async-start | bytes 2097152 | tf_op jit(solution)/shard_map/all_to_all | solution.py:40
Sparse Core Ops, SparseCore 0:
  54.3 58.2 all-gather.4
  115.7 63.2 all-gather.2
where the time goes:
time: 192 us; the launch traced here: 191 us
  blocking collectives  79.9 us (42%)
  waiting for transfers between devices  51.9 us (27%)
  local copies, waits for them, and re-layouts  25 us (13%)
  starting transfers between devices  14.4 us (8%)
  between operations  14.2 us (7%)
  other arithmetic  5.96 us (3%)
    all_to_all x2, blocking collectives, moved_by_axis(): out = lax.all_to_all(out, axes[k], k, k, tiled=True)  56.1 us
    all_to_all x1, waiting for transfers between devices, outer_step(): lax.all_to_all(delta_output, REP, split_axis=3, concat_axis=0, tiled=True)  28 us
    all_to_all x1, waiting for transfers between devices, copy_for_each(): lax.all_to_all(jnp.broadcast_to(value[None], (length, *value.shape)), axi...  23.9 us
    all_to_all x1, blocking collectives, outer_step(): lax.all_to_all(delta_latent, REP, split_axis=2, concat_axis=0, tiled=True)  23.9 us
    unnamed x22, local copies, waits for them, and re-layouts  20 us
    all_to_all x1, starting transfers between devices, outer_step(): lax.all_to_all(delta_output, REP, split_axis=3, concat_axis=0, tiled=True)  9.58 us
    all_to_all x1, starting transfers between devices, copy_for_each(): lax.all_to_all(jnp.broadcast_to(value[None], (length, *value.shape)), axi...  4.7 us
  transfers between devices with their start and end apart: 4, of which 2 were waited for; matrix products, arithmetic and copies ran while one was open for 9% of the time, Pallas kernels for 0%

commit v1 on v0

--- a/solution.py
+++ b/solution.py
@@ -67,7 +67,17 @@
 ):
     replica_count = lax.axis_size(REP)
     query_terms = core_and_chips(delta_query, (("rep_0", "rep_1"), "rep_2"), (1, 0), 2, 0)
-    latent_terms = lax.all_to_all(delta_latent, REP, split_axis=2, concat_axis=0, tiled=True)
+
+    def define_cards(x_local, mesh_ax):
+        y2 = jnp.concatenate(
+            lax.all_to_all(
+                jnp.stack(jnp.split(x_local, lax.axis_size(mesh_ax), axis=2), axis=0), mesh_ax, 0, 0
+            ),
+            axis=0,
+        )
+        return y2
+
+    latent_terms = define_cards(delta_latent, REP)
     output_terms = lax.all_to_all(delta_output, REP, split_axis=3, concat_axis=0, tiled=True)
     query_totals = jnp.sum(query_terms.astype(jnp.float32), 0)
     latent_totals = jnp.sum(latent_terms.astype(jnp.float32), 0)

time: 192 us -> 190 us (0.990)
    unnamed x22 -> x36, local copies, waits for them, and re-layouts: 20 us -> 19 us
  transfers between devices with their start and end apart: 4 -> 4, of which waited for: 2 -> 2; matrix products, arithmetic and copies ran while one was open for 9% -> 8% of each run, Pallas kernels for 0% -> 0%
where the time goes in v1:
time: 190 us; the launch traced here: 189 us
  blocking collectives  79.9 us (42%)
  waiting for transfers between devices  51.3 us (27%)
  local copies, waits for them, and re-layouts  24 us (13%)
  starting transfers between devices  14.4 us (8%)
  between operations  14.3 us (8%)
  other arithmetic  5.21 us (3%)
    all_to_all x2, blocking collectives, moved_by_axis(): out = lax.all_to_all(out, axes[k], k, k, tiled=True)  56.1 us
    all_to_all x1, waiting for transfers between devices, outer_step(): lax.all_to_all(delta_output, REP, split_axis=3, concat_axis=0, tiled=True)  28 us
    all_to_all x1, blocking collectives, define_cards(): lax.all_to_all(jnp.stack(jnp.split(x_local, lax.axis_size(mesh_ax), axis=...  23.9 us
    all_to_all x1, waiting for transfers between devices, copy_for_each(): lax.all_to_all(jnp.broadcast_to(value[None], (length, *value.shape)), axi...  23.3 us
    unnamed x36, local copies, waits for them, and re-layouts  19 us
    all_to_all x1, starting transfers between devices, outer_step(): lax.all_to_all(delta_output, REP, split_axis=3, concat_axis=0, tiled=True)  9.58 us
    all_to_all x1, starting transfers between devices, copy_for_each(): lax.all_to_all(jnp.broadcast_to(value[None], (length, *value.shape)), axi...  4.7 us
  transfers between devices with their start and end apart: 4, of which 2 were waited for; matrix products, arithmetic and copies ran while one was open for 8% of the time, Pallas kernels for 0%

profile of v1, /device:TPU:1, one launch (start us, length us, event | category | flops | bytes accessed | tf_op | source)
XLA Modules:
  0.0 189.1 jit_solution(3880137504730245485)
XLA Ops:
  7.2 0.0 copy-start.3
  7.2 6.2 %copy.43 = bf16[1,2,256,2048]{2,1,0,3:T(2,128)(2,1)} copy(bf16[1,2,256,2048]{3,2,1,0:T(8,128)(2,1)} %param.15) | data formatting | bytes 4194304 | tf_op args[6]
  13.4 0.0 copy-start.4
  13.4 9.6 %all-to-all-start.4 = ((bf16[1,2,256,2048]{2,1,0,3:T(2,128)(2,1)}), bf16[1,2,256,2048]{2,1,0,3:T(2,128)(2,1)S(1)}, u32[]{:S(2)}, u32[]{:S(2)}) async-start(bf16[1,2,256,2048]{2,1,0,3:T(2,128)(2,1)} %copy.43), calls=%async_computation.4 | async-start | bytes 4194304 | tf_op jit(solution)/shard_map/all_to_all | solution.py:81
  23.0 0.0 all-gather.5.cloned.1.call-start
  23.0 0.0 copy-done.3
  23.0 0.1 copy.44
  23.2 0.0 copy-done.4
  23.2 0.1 copy.45
  23.3 28.0 %all-to-all-done.4 = bf16[1,2,256,2048]{2,1,0,3:T(2,128)(2,1)S(1)} async-done(((bf16[1,2,256,2048]{2,1,0,3:T(2,128)(2,1)}), bf16[1,2,256,2048]{2,1,0,3:T(2,128)(2,1)S(1)}, u32[]{:S(2)}, u32[]{:S(2)}) %all-to-all-start.4) | async-done | bytes 2097184 | tf_op jit(solution)/shard_map/all_to_all | solution.py:81
  51.3 1.8 convert_reduce_fusion.1
  53.1 1.1 fusion
  54.2 0.0 all-gather.5.cloned.1.call-update
  54.2 0.0 all-gather.3.cloned.1.call-start
  54.2 2.4 %copy.40 = bf16[8,2,1,2,128,384]{5,4,0,3,2,1:T(8,128)(2,1)S(1)} copy(bf16[8,2,1,2,128,384]{5,4,1,0,3,2:T(8,128)(2,1)} %bitcast.43) | data formatting | bytes 6291456 | tf_op jit(solution)/shard_map/reshape | solution.py:26
  56.6 6.9 %all_to_all.29 = bf16[8,2,1,2,128,384]{5,4,0,3,2,1:T(8,128)(2,1)S(1)} all-to-all(bf16[8,2,1,2,128,384]{5,4,0,3,2,1:T(8,128)(2,1)S(1)} %copy.40), channel_id=1, replica_groups=mesh['rep_0'=2,'rep_1'=4,'rep_2'=2,'tp'=8] {'rep_2'}, dimensions={1} | all-to-all | bytes 6291456 | tf_op jit(solution)/shard_map/all_to_all | solution.py:28
  63.6 0.5 copy.41
  64.1 49.1 %all_to_all.30 = bf16[8,2,1,2,128,384]{5,4,1,3,2,0:T(8,128)(2,1)S(1)} all-to-all(bf16[8,2,1,2,128,384]{5,4,1,3,2,0:T(8,128)(2,1)S(1)} %copy.41), channel_id=1, replica_groups=mesh['rep_0'=2,'rep_1'=4,'rep_2'=2,'tp'=8] {'rep_0','rep_1'}, dimensions={0} | all-to-all | bytes 6291456 | tf_op jit(solution)/shard_map/all_to_all | solution.py:28
  113.2 0.0 copy-start.1
  113.2 0.0 copy-start.2
  113.2 0.0 copy-start
  113.2 0.4 convert_reduce_fusion
  113.7 0.6 copy-done.1
  114.2 0.1 copy-done.2
  114.3 1.0 fusion.2
  115.4 0.0 copy-start.5
  115.4 0.0 copy-start.6
  115.4 0.0 all-gather.3.cloned.1.call-update
  115.4 0.0 copy-done
  115.7 23.9 %all_to_all.31 = bf16[16,1,2,32,512]{4,3,2,1,0:T(8,128)(2,1)S(1)} all-to-all(bf16[16,1,2,32,512]{4,3,2,1,0:T(8,128)(2,1)S(1)} %bitcast_dynamic-update-slice_fusion), channel_id=1, replica_groups=mesh['rep_0'=2,'rep_1'=4,'rep_2'=2,'tp'=8] {'rep_0','rep_1','rep_2'}, dimensions={0} | all-to-all | bytes 2097152 | tf_op jit(solution)/shard_map/all_to_all | solution.py:73
  139.5 0.1 convert_reduce_fusion.2
  139.7 0.0 copy-done.5
  139.7 0.0 copy-done.6
  139.7 0.7 fusion.1
  140.4 1.1 broadcast_in_dim.2
  141.5 4.7 %all-to-all-start.3 = ((bf16[16,2,32,512]{3,2,1,0:T(8,128)(2,1)}), bf16[16,2,32,512]{3,2,1,0:T(8,128)(2,1)S(1)}, u32[]{:S(2)}, u32[]{:S(2)}) async-start(bf16[16,2,32,512]{3,2,1,0:T(8,128)(2,1)} %broadcast_in_dim.2), calls=%async_computation.3 | async-start | bytes 2097152 | tf_op jit(solution)/shard_map/all_to_all | solution.py:40
  146.2 0.8 copy.47
  147.1 0.8 copy.48
  147.9 23.3 %all-to-all-done.3 = bf16[16,2,32,512]{3,2,1,0:T(8,128)(2,1)S(1)} async-done(((bf16[16,2,32,512]{3,2,1,0:T(8,128)(2,1)}), bf16[16,2,32,512]{3,2,1,0:T(8,128)(2,1)S(1)}, u32[]{:S(2)}, u32[]{:S(2)}) %all-to-all-start.3) | async-done | bytes 1048608 | tf_op jit(solution)/shard_map/all_to_all | solution.py:40
  171.2 1.0 copy.42
  172.3 0.0 all-gather.5.cloned.1.call-done
  172.3 6.2 %copy.46 = bf16[2,256,2048]{2,1,0:T(8,128)(2,1)} copy(bf16[2,256,2048]{1,0,2:T(2,128)(2,1)} %all-gather.5.cloned.1.call-done) | data formatting | bytes 4194304
  178.4 0.0 all-gather.3.cloned.1.call-done
  178.4 3.9 %copy.67 = bf16[2,2048,384]{2,1,0:T(8,128)(2,1)} copy(bf16[2,2048,384]{2,1,0:T(8,128)(2,1)} %all-gather.3.cloned.1.call-done) | data formatting | bytes 6291456
  (16 shorter events, 0.1 us)
Async XLA Ops:
  7.2 15.8 %copy-start.3 = (f32[2,256,128]{2,1,0:T(8,128)S(1)}, f32[2,256,128]{2,1,0:T(8,128)}, u32[]{:S(2)}) copy-start(f32[2,256,128]{2,1,0:T(8,128)} %param.17) | copy-start | bytes 786436
  13.4 9.8 %copy-start.4 = (f32[2,256,128]{2,1,0:T(8,128)S(1)}, f32[2,256,128]{2,1,0:T(8,128)}, u32[]{:S(2)}) copy-start(f32[2,256,128]{2,1,0:T(8,128)} %param.16) | copy-start | bytes 786436
  13.4 37.9 %all-to-all-start.4 = ((bf16[1,2,256,2048]{2,1,0,3:T(2,128)(2,1)}), bf16[1,2,256,2048]{2,1,0,3:T(2,128)(2,1)S(1)}, u32[]{:S(2)}, u32[]{:S(2)}) async-start(bf16[1,2,256,2048]{2,1,0,3:T(2,128)(2,1)} %copy.43), calls=%async_computation.4 | async-start | bytes 4194304 | tf_op jit(solution)/shard_map/all_to_all | solution.py:81
  23.0 149.3 %all-gather.5.cloned.1.call-start = ((), (), s32[]{:S(2)}) async-start(), calls=%async_computation.6 | async-start | bytes 2228224 | tf_op jit(solution)/shard_map/all_gather | solution.py:94
  54.2 124.2 %all-gather.3.cloned.1.call-start = ((), (), s32[]{:S(2)}) async-start(), calls=%async_computation.5 | async-start | bytes 3342336 | tf_op jit(solution)/shard_map/all_gather | solution.py:92
  113.2 1.0 copy-start.1
  113.2 1.1 copy-start.2
  113.2 2.2 %copy-start = (bf16[1,2,512,512]{3,2,1,0:T(8,128)(2,1)S(1)}, bf16[1,2,512,512]{3,2,1,0:T(8,128)(2,1)}, u32[]{:S(2)}) copy-start(bf16[1,2,512,512]{3,2,1,0:T(8,128)(2,1)} %param.12) | copy-start | bytes 3145732
  115.4 24.3 %copy-start.5 = (f32[2,32,512]{2,1,0:T(8,128)S(1)}, f32[2,32,512]{2,1,0:T(8,128)}, u32[]{:S(2)}) copy-start(f32[2,32,512]{2,1,0:T(8,128)} %param.13) | copy-start | bytes 393220
  115.4 24.3 %copy-start.6 = (f32[2,32,512]{2,1,0:T(8,128)S(1)}, f32[2,32,512]{2,1,0:T(8,128)}, u32[]{:S(2)}) copy-start(f32[2,32,512]{2,1,0:T(8,128)} %param.14) | copy-start | bytes 393220
  141.5 29.7 %all-to-all-start.3 = ((bf16[16,2,32,512]{3,2,1,0:T(8,128)(2,1)}), bf16[16,2,32,512]{3,2,1,0:T(8,128)(2,1)S(1)}, u32[]{:S(2)}, u32[]{:S(2)}) async-start(bf16[16,2,32,512]{3,2,1,0:T(8,128)(2,1)} %broadcast_in_dim.2), calls=%async_computation.3 | async-start | bytes 2097152 | tf_op jit(solution)/shard_map/all_to_all | solution.py:40
Sparse Core Ops, SparseCore 0:
  54.3 58.2 all-gather.4
  115.7 62.1 all-gather.2
